TPU v7x, 32 devices: a whole 2x2x4 slice. The times are simulated.
32 devices in a mesh: section: 2 (over x), dp: 16 (over z, y, core).
Axes of the slice: x: 2, y: 2, z: 4, core: 2. Of those that a mesh axis runs over, the one named last changes fastest.
Arguments:
- ln_input: bfloat16 [2, 2048, 12288], P('section', 'dp'), may hold values from -6 to 6
- ln_grad: bfloat16 [2, 2048, 12288], P('section', 'dp'), may hold values from -6 to 6
- top_grad: bfloat16 [2, 2048, 12288], P('section', 'dp'), may hold values from -6 to 6
- ln_gain: float32 [2, 12288], P('section'), may hold values from 0.1 to 1.9
- hidden: bfloat16 [2, 2048, 32], P('section', 'dp'), may hold values from -8 to 8
- master: float32 [2, 32, 12288], P('section', 'dp'), may hold values from -6 to 6
- moment: float32 [2, 32, 12288], P('section', 'dp'), may hold values from -6 to 6
- second: float32 [2, 32, 12288], P('section', 'dp'), may hold values from 0.1 to 4
Outputs:
- new_master: float32 [2, 32, 12288], P('section', 'dp')
- new_moment: float32 [2, 32, 12288], P('section', 'dp')
- new_second: float32 [2, 32, 12288], P('section', 'dp')
- weights: bfloat16 [2, 32, 12288], P('section')
All inputs are finite; a program needn't handle non-finite values.
Results may differ from a plain program's by a relative error of at most 0.0078.
Values may be sent and summed in bfloat16 or wider, within the bound.
A program may use at most 64 MiB of HBM per device.

v0:
```python
import jax
import jax.numpy as jnp
from jax import lax
from jax.sharding import PartitionSpec as P

STEP = 20


def shifted(value, axis, steps):
    count = lax.axis_size(axis)
    first, last = (max(0, -steps), min(count, count - steps))
    return lax.ppermute(value, axis, [(source, source + steps) for source in range(first, last)])


def layer_back(ln_input, ln_grad, top_grad, ln_gain):
    values = ln_input.astype(jnp.float32)
    row_mean = jnp.mean(values, axis=-1, keepdims=True)
    centred = values - row_mean
    inv_std = 1.0 / jnp.sqrt(jnp.mean(centred * centred, axis=-1, keepdims=True) + 1e-05)
    normed = centred * inv_std
    scaled = ln_grad.astype(jnp.float32) * ln_gain[:, None, :]
    inner = (
        scaled
        - jnp.mean(scaled, axis=-1, keepdims=True)
        - normed * jnp.mean(scaled * normed, axis=-1, keepdims=True)
    )
    return (top_grad.astype(jnp.float32) + inner * inv_std).astype(jnp.bfloat16)


def adam_update(grad, master, moment, second):
    new_moment = 0.9 * moment + 0.1 * grad
    new_second = 0.95 * second + 0.05 * grad * grad
    first_fix = 1.0 - 0.9**STEP
    second_fix = 1.0 - 0.95**STEP
    update = new_moment / first_fix / (jnp.sqrt(new_second / second_fix) + 1e-08)
    new_master = master - 0.05 * (update + 0.1 * master)
    return (new_master, new_moment, new_second)


def term_maker(columns, received):
    return lax.dot_general(
        columns, received, (((0,), (0,)), ((), ())), preferred_element_type=jnp.float32
    )


def owner_columns(columns, group_size, row_dev, first, last_row):
    tokens_here = columns.shape[0]
    grouped = columns.reshape(tokens_here, group_size, row_dev)
    return grouped.reshape(tokens_here, group_size * (last_row - first))


def shards(ln_input, ln_grad, top_grad, ln_gain, hidden, master, moment, second):
    passed = layer_back(ln_input, ln_grad, top_grad, ln_gain)
    is_last = lax.axis_index("section") == lax.axis_size("section") - 1
    row_dev = master.shape[1]
    width = master.shape[2]
    group_size = lax.axis_size("dp")
    own_cols = hidden[0]
    lower_cols = shifted(hidden, "section", 1)[0]
    received = passed[0]
    bounds = (0, row_dev)
    first, last_row = bounds
    count = last_row - first
    below = owner_columns(lower_cols, group_size, row_dev, first, last_row)
    mine = owner_columns(own_cols, group_size, row_dev, first, last_row)
    lower_share = lax.psum_scatter(
        term_maker(below, received), "dp", scatter_dimension=0, tiled=True
    )
    own_share = lax.psum_scatter(
        term_maker(mine, top_grad[0]), "dp", scatter_dimension=0, tiled=True
    )
    from_above = shifted(lower_share, "section", -1)
    grad = jnp.where(is_last, own_share, from_above)
    state = adam_update(
        grad, master[0, first:last_row], moment[0, first:last_row], second[0, first:last_row]
    )
    masters = state[0]
    moments = state[1]
    seconds = state[2]
    pieces = lax.all_gather(state[0].astype(jnp.bfloat16), "dp", axis=0, tiled=True)
    gathered = pieces.reshape(group_size, count, width)
    weights = gathered.reshape(group_size * row_dev, width)
    return (masters[None], moments[None], seconds[None], weights[None])


def solution(mesh):
    return jax.shard_map(
        shards,
        mesh=mesh,
        in_specs=(
            P("section", "dp", None),
            P("section", "dp", None),
            P("section", "dp", None),
            P("section", None),
            P("section", "dp", None),
            P("section", "dp", None),
            P("section", "dp", None),
            P("section", "dp", None),
        ),
        out_specs=(
            P("section", "dp", None),
            P("section", "dp", None),
            P("section", "dp", None),
            P("section", None, None),
        ),
        check_vma=False,
    )
```

profile of v0, /device:TPU:0, one launch (start us, length us, event | category | flops | bytes accessed | tf_op | source)
XLA Modules:
  0.0 168.3 jit_solution(10690842517051221924)
XLA Ops:
  7.2 0.0 copy-start
  7.2 0.0 all-reduce.5.cloned.1.call-start
  7.2 0.0 copy-start.2
  7.2 5.1 %collective-permute-start = (bf16[1,128,32]{1,2,0:T(8,128)(2,1)}, bf16[1,128,32]{1,2,0:T(8,128)(2,1)S(1)}, u32[]{:S(2)}, u32[]{:S(2)}) collective-permute-start(bf16[1,128,32]{1,2,0:T(8,128)(2,1)} %param.12), channel_id=1, source_target_pairs={{0,16},{1,17},{2,18},{3,19},{4,20},{5,21},{6,22},{7,23},{8,24},{9,... | collective-permute-start | bytes 24584 | tf_op jit(solution)/shard_map/ppermute | solution.py:12
  12.4 2.4 %convert_reduce_fusion = f32[128]{0:T(128)S(1)} fusion(bf16[1,128,12288]{2,1,0:T(8,128)(2,1)} %param.8), kind=kLoop, calls=%fused_computation.2 | loop fusion | flops 3145600 | bytes 3146240 | tf_op jit(solution)/shard_map/reduce_sum | solution.py:17
  14.8 0.0 copy-done
  14.8 1.0 fusion.9
  15.8 0.0 copy-start.1
  15.8 0.0 copy-start.6
  15.8 0.0 copy-done.2
  15.8 2.6 %fusion.12 = f32[32,12288]{1,0:T(8,128)} fusion(bf16[1,128,12288]{2,1,0:T(8,128)(2,1)S(1)} %copy-done.2, bf16[1,128,32]{1,2,0:T(8,128)(2,1)} %param.12), kind=kOutput, calls=%fused_computation.16 | convolution fusion | flops 100663296 | bytes 4726784 | tf_op jit(solution)/shard_map/dot_general | solution.py:41
  18.4 0.0 copy-done.1
  18.4 0.0 copy-done.6
  18.4 2.1 %fusion.10 = (f32[128]{0:T(128)S(1)}, f32[128]{0:T(128)S(1)}) fusion(bf16[1,128,12288]{2,1,0:T(8,128)(2,1)S(1)} %copy-done.1, f32[12288]{0:T(1024)S(1)} %bitcast.40, f32[128]{0:T(128)S(1)} %add_rsqrt_fusion, f32[128]{0:T(128)S(1)} %broadcast_multiply_fusion.1, bf16[1,128,12288]{2,1,0:T(8,128)(2,1)S(1)} %copy-done), kind=kLoop, calls=%fused_computation.14 | loop fusion | flops 12582656 | bytes 6342656 | tf_op jit(solution)/shard_map/reduce_sum | solution.py:24
  20.5 0.0 collective-permute-done
  20.5 4.0 %convolution_bitcast_fusion = f32[32,12288]{1,0:T(8,128)} fusion(bf16[1,128,12288]{2,1,0:T(8,128)(2,1)S(1)} %copy-done, bf16[1,128,12288]{2,1,0:T(8,128)(2,1)S(1)} %copy-done.1, bf16[1,128,12288]{2,1,0:T(8,128)(2,1)S(1)} %copy-done.2, f32[128]{0:T(128)S(1)} %get-tuple-element.12, f32[128]{0:T(128)S(1)} %add_rsqrt_fusion, f32[128]{0:T(128)S(1)} %broadcast_multiply_fusion.1, ...), kind=kOutput, calls=%fused_computation | convolution fusion | flops 119537664 | bytes 11069440 | tf_op jit(solution)/shard_map/dot_general | solution.py:41
  24.4 0.0 copy-start.7
  24.4 0.0 copy-start.3
  24.4 0.0 copy-start.4
  24.5 0.0 copy-start.5
  24.5 0.0 all-reduce.5.cloned.1.call-update
  24.5 0.6 copy-done.7
  25.1 0.6 dynamic-slice
  26.3 102.7 %all-reduce.5.cloned.1.call-done = (f32[32,12288]{1,0:T(8,128)}, f32[32,12288]{1,0:T(8,128)}) async-done(((f32[32,12288]{1,0:T(8,128)}, f32[32,12288]{1,0:T(8,128)}), (f32[32,12288]{1,0:T(8,128)}, f32[32,12288]{1,0:T(8,128)})) %all-reduce.5.cloned.1.call-update) | async-done | bytes 3145744
  129.0 1.0 constant_dynamic-slice_fusion
  130.1 1.3 collective-permute-start.1
  131.4 5.2 %collective-permute-done.1 = f32[2,12288]{1,0:T(2,128)S(1)} collective-permute-done((f32[2,12288]{1,0:T(2,128)S(1)}, f32[2,12288]{1,0:T(2,128)S(1)}, u32[]{:S(2)}, u32[]{:S(2)}) %collective-permute-start.1) | collective-permute-done | bytes 98336 | tf_op jit(solution)/shard_map/ppermute | solution.py:12
  136.6 0.0 copy-done.3
  136.6 0.0 copy-done.4
  136.6 0.0 copy-done.5
  136.6 2.1 %convert_bitcast_fusion = (bf16[1,2,12288]{2,1,0:T(2,128)(2,1)S(1)}, f32[2,12288]{1,0:T(2,128)}, f32[2,12288]{1,0:T(2,128)}, f32[2,12288]{1,0:T(2,128)}) fusion(f32[1,2,12288]{2,1,0:T(2,128)S(1)} %copy-done.3, f32[2,12288]{1,0:T(2,128)S(1)} %collective-permute-done.1, f32[32,12288]{1,0:T(8,128)} %get-tuple-element.7, u32[]{:T(128)S(6)} %multiply.30, ...), kind=kLoop, calls=%fused_computation.26 | loop fusion | flops 417792 | bytes 835589
  138.6 21.7 %all-gather = bf16[16,2,12288]{2,1,0:T(2,128)(2,1)S(1)} all-gather(bf16[1,2,12288]{2,1,0:T(2,128)(2,1)S(1)} %get-tuple-element.8), channel_id=1, replica_groups=mesh['section'=2,'dp'=16] {'dp'}, dimensions={0}, use_global_device_ids=true | all-gather | bytes 835584 | tf_op jit(solution)/shard_map/all_gather | solution.py:80
  160.3 1.2 broadcast_in_dim_reshape_reshape.3
  (3 shorter events, 0.0 us)
Async XLA Ops:
  7.2 7.6 %copy-start = (bf16[1,128,12288]{2,1,0:T(8,128)(2,1)S(1)}, bf16[1,128,12288]{2,1,0:T(8,128)(2,1)}, u32[]{:S(2)}) copy-start(bf16[1,128,12288]{2,1,0:T(8,128)(2,1)} %param.8) | copy-start | bytes 9437188
  7.2 121.8 %all-reduce.5.cloned.1.call-start = ((), (), s32[]{:S(2)}) async-start(), calls=%async_computation | async-start | bytes 6291456
  7.2 8.6 %copy-start.2 = (bf16[1,128,12288]{2,1,0:T(8,128)(2,1)S(1)}, bf16[1,128,12288]{2,1,0:T(8,128)(2,1)}, u32[]{:S(2)}) copy-start(bf16[1,128,12288]{2,1,0:T(8,128)(2,1)} %param.10) | copy-start | bytes 9437188
  7.2 13.2 %collective-permute-start = (bf16[1,128,32]{1,2,0:T(8,128)(2,1)}, bf16[1,128,32]{1,2,0:T(8,128)(2,1)S(1)}, u32[]{:S(2)}, u32[]{:S(2)}) collective-permute-start(bf16[1,128,32]{1,2,0:T(8,128)(2,1)} %param.12), channel_id=1, source_target_pairs={{0,16},{1,17},{2,18},{3,19},{4,20},{5,21},{6,22},{7,23},{8,24},{9,... | collective-permute-start | bytes 24584 | tf_op jit(solution)/shard_map/ppermute | solution.py:12
  15.8 2.6 %copy-start.1 = (bf16[1,128,12288]{2,1,0:T(8,128)(2,1)S(1)}, bf16[1,128,12288]{2,1,0:T(8,128)(2,1)}, u32[]{:S(2)}) copy-start(bf16[1,128,12288]{2,1,0:T(8,128)(2,1)} %param.9) | copy-start | bytes 9437188
  15.8 2.6 %copy-start.6 = (f32[1,12288]{1,0:T(1,128)S(1)}, f32[1,12288]{1,0:T(1,128)}, u32[]{:S(2)}) copy-start(f32[1,12288]{1,0:T(1,128)} %param.11) | copy-start | bytes 147460
  24.4 0.7 copy-start.7
  24.4 112.1 %copy-start.3 = (f32[1,2,12288]{2,1,0:T(2,128)S(1)}, f32[1,2,12288]{2,1,0:T(2,128)}, u32[]{:S(2)}) copy-start(f32[1,2,12288]{2,1,0:T(2,128)} %param.13) | copy-start | bytes 294916
  24.4 112.1 %copy-start.4 = (f32[1,2,12288]{2,1,0:T(2,128)S(1)}, f32[1,2,12288]{2,1,0:T(2,128)}, u32[]{:S(2)}) copy-start(f32[1,2,12288]{2,1,0:T(2,128)} %param.14) | copy-start | bytes 294916
  24.5 112.1 %copy-start.5 = (f32[1,2,12288]{2,1,0:T(2,128)S(1)}, f32[1,2,12288]{2,1,0:T(2,128)}, u32[]{:S(2)}) copy-start(f32[1,2,12288]{2,1,0:T(2,128)} %param.15) | copy-start | bytes 294916
  130.1 6.5 %collective-permute-start.1 = (f32[2,12288]{1,0:T(2,128)S(1)}, f32[2,12288]{1,0:T(2,128)S(1)}, u32[]{:S(2)}, u32[]{:S(2)}) collective-permute-start(f32[2,12288]{1,0:T(2,128)S(1)} %constant_dynamic-slice_fusion), channel_id=1, source_target_pairs={{16,0},{17,1},{18,2},{19,3},{20,4},{21,5},{22,6},{23,7},{24,8},{25... | collective-permute-start | bytes 294920 | tf_op jit(solution)/shard_map/ppermute | solution.py:12
Sparse Core Ops, SparseCore 0:
  24.6 104.3 all-reduce.4
where the time goes:
time: 169 us; the launch traced here: 168 us
  waiting for transfers between devices  108 us (64%)
  blocking collectives  21.7 us (13%)
  between operations  14.8 us (9%)
  other arithmetic  7.52 us (4%)
  matrix products  6.54 us (4%)
  starting transfers between devices  6.47 us (4%)
  local copies, waits for them, and re-layouts  3.43 us (2%)
    unnamed x2, waiting for transfers between devices  103 us
    all_gather x1, blocking collectives, shards(): lax.all_gather(state[0].astype(jnp.bfloat16), 'dp', axis=0, tiled=True)  21.7 us
    dot_general x2, matrix products, term_maker(): lax.dot_general(columns, received, (((0,), (0,)), ((), ())), preferred_el...  6.54 us
    ppermute x2, starting transfers between devices, shifted(): lax.ppermute(value, axis, [(source, source + steps) for source in range(f...  6.43 us
    ppermute x2, waiting for transfers between devices, shifted(): lax.ppermute(value, axis, [(source, source + steps) for source in range(f...  5.21 us
  transfers between devices with their start and end apart: 3, of which 2 were waited for; matrix products, arithmetic and copies ran while one was open for 5% of the time, Pallas kernels for 0%

commit v1 on v0

v1 whole, which is shorter than its diff:
```python
import functools

import jax
import jax.numpy as jnp
from jax import lax
from jax.experimental import pallas as pl
from jax.experimental.pallas import tpu as pltpu
from jax.sharding import PartitionSpec as P

STEP = 20
CORES = 2
CHUNKS = 4
LANES = 128
MESH = pl.DeviceIdType.MESH


def adam_update(grad, master, moment, second):
    new_moment = 0.9 * moment + 0.1 * grad
    new_second = 0.95 * second + 0.05 * grad * grad
    first_fix = 1.0 - 0.9**STEP
    second_fix = 1.0 - 0.95**STEP
    update = new_moment / first_fix / (jnp.sqrt(new_second / second_fix) + 1e-08)
    new_master = master - 0.05 * (update + 0.1 * master)
    return (new_master, new_moment, new_second)


def kernel(
    sections,
    group,
    ln_input_hbm,
    ln_grad_hbm,
    top_grad_hbm,
    gain_hbm,
    hidden_hbm,
    master_hbm,
    moment_hbm,
    second_hbm,
    new_master_ref,
    new_moment_ref,
    new_second_ref,
    weights_ref,
    x_ref,
    g_ref,
    t_ref,
    gain_ref,
    hidden_ref,
    lower_ref,
    state_ref,
    stats_ref,
    mine_ref,
    theirs_ref,
    partner_ref,
    stage_ref,
    recv_ref,
    load_sem,
    state_sem,
    hid_send,
    hid_recv,
    pair_send,
    pair_recv,
    rs_send,
    rs_recv,
    ag_send,
    ag_recv,
    fw_send,
    fw_recv,
):
    tokens, width = x_ref.shape
    rows = hidden_ref.shape[0]
    row_dev = new_master_ref.shape[0]
    chips = group // CORES
    half = rows // CORES
    cols_chunk = width // CHUNKS
    blocks = 4
    block_rows = tokens // blocks

    sec = lax.axis_index("section")
    me = lax.axis_index("dp")
    core = lax.rem(me, CORES)
    chip = lax.div(me, CORES)
    partner = chip * CORES + (1 - core)
    has_lower = sec > 0
    has_upper = sec < sections - 1
    is_last = sec == sections - 1

    def chip_dev(index):
        return index * CORES + core

    def other_chip(step):
        return lax.rem(chip + step, chips)

    barrier = pltpu.get_barrier_semaphore()
    pl.semaphore_signal(barrier, inc=1, device_id=(sec, partner), device_id_type=MESH)
    for step in range(1, chips):
        pl.semaphore_signal(
            barrier, inc=1, device_id=(sec, chip_dev(other_chip(step))), device_id_type=MESH
        )

    @pl.when(has_lower)
    def _():
        for step in range(chips):
            pl.semaphore_signal(
                barrier,
                inc=1,
                device_id=(sec - 1, chip_dev(other_chip(step))),
                device_id_type=MESH,
            )

    @pl.when(has_upper)
    def _():
        for step in range(chips):
            pl.semaphore_signal(
                barrier,
                inc=1,
                device_id=(sec + 1, chip_dev(other_chip(step))),
                device_id_type=MESH,
            )

    def row_block(b):
        return pl.ds(b * block_rows, block_rows)

    x_loads = [
        pltpu.make_async_copy(
            ln_input_hbm.at[row_block(b)], x_ref.at[row_block(b)], load_sem.at[b]
        )
        for b in range(blocks)
    ]
    g_loads = [
        pltpu.make_async_copy(
            ln_grad_hbm.at[row_block(b)], g_ref.at[row_block(b)], load_sem.at[blocks + b]
        )
        for b in range(blocks)
    ]
    t_load = pltpu.make_async_copy(top_grad_hbm, t_ref, load_sem.at[2 * blocks])
    gain_load = pltpu.make_async_copy(gain_hbm, gain_ref, load_sem.at[2 * blocks + 1])
    hidden_load = pltpu.make_async_copy(hidden_hbm, hidden_ref, load_sem.at[2 * blocks + 2])
    state_loads = [
        pltpu.make_async_copy(source, state_ref.at[i], state_sem.at[i])
        for i, source in enumerate((master_hbm, moment_hbm, second_hbm))
    ]
    hidden_copy = pltpu.make_async_remote_copy(
        src_ref=hidden_hbm,
        dst_ref=lower_ref,
        send_sem=hid_send,
        recv_sem=hid_recv,
        device_id=(lax.rem(sec + 1, sections), me),
        device_id_type=MESH,
    )

    @pl.when(has_lower)
    def _():
        gain_load.start()
        for b in range(blocks):
            x_loads[b].start()
            g_loads[b].start()

    @pl.when(has_lower | is_last)
    def _():
        t_load.start()

    @pl.when(is_last)
    def _():
        hidden_load.start()

    for load in state_loads:
        load.start()

    peers = (
        chips
        + jnp.where(has_lower, chips, 0)
        + jnp.where(has_upper, chips, 0)
    )
    pl.semaphore_wait(barrier, peers)

    @pl.when(has_upper)
    def _():
        hidden_copy.start()

    def columns(start, size):
        return pl.ds(pl.multiple_of(start, LANES), size)

    def arranged(source):
        to = lax.broadcasted_iota(jnp.int32, (rows, rows), 0)
        at = lax.broadcasted_iota(jnp.int32, (rows, rows), 1)
        within = lax.rem(to, half)
        which = jnp.where(to < half, core, 1 - core)
        wanted = (lax.div(within, row_dev) * CORES + which) * row_dev + lax.rem(within, row_dev)
        select = jnp.where(at == wanted, 1.0, 0.0).astype(jnp.bfloat16)
        return lax.dot_general(
            select, source[...], (((1,), (0,)), ((), ())), preferred_element_type=jnp.float32
        ).astype(jnp.bfloat16)

    def pair_copy(path, q):
        cols = pl.ds(q * cols_chunk, cols_chunk)
        return pltpu.make_async_remote_copy(
            src_ref=theirs_ref.at[path, :, cols],
            dst_ref=partner_ref.at[path, :, cols],
            send_sem=pair_send.at[path, q],
            recv_sem=pair_recv.at[path, q],
            device_id=(sec, partner),
            device_id_type=MESH,
        )

    def share_copy(path, q, target):
        cols = pl.ds(q * cols_chunk, cols_chunk)
        to_sec = lax.rem(sec + sections - 1, sections) if path == 0 else sec
        return pltpu.make_async_remote_copy(
            src_ref=stage_ref.at[path, target, :, cols],
            dst_ref=recv_ref.at[chip, :, cols],
            send_sem=rs_send.at[path, target, q],
            recv_sem=rs_recv.at[chip, q],
            device_id=(to_sec, chip_dev(target)),
            device_id_type=MESH,
        )

    def own_copy(q):
        cols = pl.ds(q * cols_chunk, cols_chunk)
        return pltpu.make_async_copy(
            stage_ref.at[1, chip, :, cols], recv_ref.at[chip, :, cols], rs_recv.at[chip, q]
        )

    sub = 256

    def product(path, q, lhs, make):
        def body(i, carry):
            cols = columns(q * cols_chunk + i * sub, sub)
            term = jnp.dot(lhs, make(cols), preferred_element_type=jnp.float32)
            mine_ref[path, :, cols] = term[:half]
            theirs_ref[path, :, cols] = term[half:]
            return carry

        lax.fori_loop(0, cols_chunk // sub, body, 0)
        pair_copy(path, q).start()

    def reduce_send(path, q):
        pair_copy(path, q).wait_recv()
        part = 512

        def body(i, carry):
            cols = columns(q * cols_chunk + i * part, part)
            total = (mine_ref[path, :, cols] + partner_ref[path, :, cols]).astype(jnp.bfloat16)
            for k in range(chips):
                stage_ref[path, k, :, cols] = total[k * row_dev : (k + 1) * row_dev]
            return carry

        lax.fori_loop(0, cols_chunk // part, body, 0)
        if path == 1:
            own_copy(q).start()
        for step in range(1 if path == 1 else 0, chips):
            share_copy(path, q, other_chip(step)).start()

    @pl.when(has_lower)
    def _():
        gain_load.wait()
        sub_rows = 16
        span = 1536

        def fold(value):
            parts = [value[:, i * LANES : (i + 1) * LANES] for i in range(span // LANES)]
            while len(parts) > 1:
                parts = [
                    parts[i] + parts[i + 1] if i + 1 < len(parts) else parts[i]
                    for i in range(0, len(parts), 2)
                ]
            return parts[0]

        def statistics(r, carry):
            at = pl.ds(pl.multiple_of(r * sub_rows, sub_rows), sub_rows)
            zero = jnp.zeros((sub_rows, LANES), jnp.float32)

            def first(i, sums):
                cols = columns(i * span, span)
                values = x_ref[at, cols].astype(jnp.float32)
                scaled = g_ref[at, cols].astype(jnp.float32) * gain_ref[:, cols]
                return (sums[0] + fold(values), sums[1] + fold(scaled))

            sums = lax.fori_loop(0, width // span, first, (zero, zero))
            mean = jnp.sum(sums[0], axis=-1, keepdims=True) / width
            mean_scaled = jnp.sum(sums[1], axis=-1, keepdims=True) / width

            def second(i, sums):
                cols = columns(i * span, span)
                centred = x_ref[at, cols].astype(jnp.float32) - mean
                scaled = g_ref[at, cols].astype(jnp.float32) * gain_ref[:, cols]
                return (sums[0] + fold(centred * centred), sums[1] + fold(scaled * centred))

            sums = lax.fori_loop(0, width // span, second, (zero, zero))
            var = jnp.sum(sums[0], axis=-1, keepdims=True) / width
            inv_std = 1.0 / jnp.sqrt(var + 1e-05)
            along = jnp.sum(sums[1], axis=-1, keepdims=True) / width * inv_std
            full = (sub_rows, LANES)
            stats_ref[0, at, :] = jnp.broadcast_to(mean, full)
            stats_ref[1, at, :] = jnp.broadcast_to(mean_scaled, full)
            stats_ref[2, at, :] = jnp.broadcast_to(along * inv_std, full)
            stats_ref[3, at, :] = jnp.broadcast_to(inv_std, full)
            return carry

        per_block = block_rows // sub_rows
        for b in range(blocks):
            x_loads[b].wait()
            g_loads[b].wait()
            lax.fori_loop(b * per_block, (b + 1) * per_block, statistics, 0)

    @pl.when(has_lower | is_last)
    def _():
        t_load.wait()

    @pl.when(has_lower)
    def _():
        hidden_copy.wait_recv()
        lhs = arranged(lower_ref)

        def passed(cols):
            def wide(i):
                return jnp.concatenate([stats_ref[i]] * (sub // LANES), axis=1)

            centred = x_ref[:, cols].astype(jnp.float32) - wide(0)
            scaled = g_ref[:, cols].astype(jnp.float32) * gain_ref[:, cols]
            inner = (scaled - wide(1)) - centred * wide(2)
            return (t_ref[:, cols].astype(jnp.float32) + inner * wide(3)).astype(jnp.bfloat16)

        for q in range(CHUNKS):
            product(0, q, lhs, passed)
            if q:
                reduce_send(0, q - 1)
        reduce_send(0, CHUNKS - 1)

    @pl.when(is_last)
    def _():
        hidden_load.wait()
        lhs = arranged(hidden_ref)
        for q in range(CHUNKS):
            product(1, q, lhs, lambda cols: t_ref[:, cols])
            if q:
                reduce_send(1, q - 1)
        reduce_send(1, CHUNKS - 1)

    def gather_copy(q, source, target):
        cols = pl.ds(q * cols_chunk, cols_chunk)
        return pltpu.make_async_remote_copy(
            src_ref=weights_ref.at[chip_dev(source), :, cols],
            dst_ref=weights_ref.at[chip_dev(source), :, cols],
            send_sem=ag_send.at[target, q],
            recv_sem=ag_recv.at[source, q],
            device_id=(sec, chip_dev(target)),
            device_id_type=MESH,
        )

    def forward_copy(q, source):
        cols = pl.ds(q * cols_chunk, cols_chunk)
        return pltpu.make_async_remote_copy(
            src_ref=weights_ref.at[chip_dev(source), :, cols],
            dst_ref=weights_ref.at[chip_dev(source), :, cols],
            send_sem=fw_send.at[source, q],
            recv_sem=fw_recv.at[source, q],
            device_id=(sec, partner),
            device_id_type=MESH,
        )

    for load in state_loads:
        load.wait()

    for q in range(CHUNKS):
        cols = pl.ds(q * cols_chunk, cols_chunk)
        for k in range(chips):
            pltpu.make_async_copy(
                recv_ref.at[k, :, cols], recv_ref.at[k, :, cols], rs_recv.at[k, q]
            ).wait()
        part = 512

        def update(i, carry):
            at = columns(q * cols_chunk + i * part, part)
            grad = jnp.sum(recv_ref[:, :, at].astype(jnp.float32), axis=0)
            masters, moments, seconds = adam_update(
                grad, state_ref[0, :, at], state_ref[1, :, at], state_ref[2, :, at]
            )
            new_master_ref[:, at] = masters
            new_moment_ref[:, at] = moments
            new_second_ref[:, at] = seconds
            weights_ref[me, :, at] = masters.astype(jnp.bfloat16)
            return carry

        lax.fori_loop(0, cols_chunk // part, update, 0)
        for step in range(1, chips):
            gather_copy(q, chip, other_chip(step)).start()
        forward_copy(q, chip).start()

    for q in range(CHUNKS):
        for step in range(1, chips):
            source = other_chip(step)
            gather_copy(q, source, chip).wait_recv()
            forward_copy(q, source).start()

    for q in range(CHUNKS):
        for step in range(chips):
            source = other_chip(step)
            forward_copy(q, source).wait()
            if step:
                gather_copy(q, chip, source).wait_send()

    def finish(path):
        for q in range(CHUNKS):
            pair_copy(path, q).wait_send()
            for step in range(1 if path == 1 else 0, chips):
                share_copy(path, q, other_chip(step)).wait_send()

    @pl.when(has_lower)
    def _():
        finish(0)

    @pl.when(is_last)
    def _():
        finish(1)

    @pl.when(has_upper)
    def _():
        hidden_copy.wait_send()


def solution(mesh):
    sections = mesh.shape["section"]
    group = mesh.shape["dp"]
    chips = group // CORES

    def step(ln_input, ln_grad, top_grad, ln_gain, hidden, master, moment, second):
        tokens, width = ln_input.shape[1:]
        rows = hidden.shape[2]
        row_dev = master.shape[1]
        half = rows // CORES
        any_space = pl.BlockSpec(memory_space=pl.ANY)
        vmem = pl.BlockSpec(memory_space=pltpu.VMEM)
        state = jax.ShapeDtypeStruct((row_dev, width), jnp.float32)
        dma = pltpu.SemaphoreType.DMA
        outs = pl.pallas_call(
            functools.partial(kernel, sections, group),
            out_shape=(
                state,
                state,
                state,
                jax.ShapeDtypeStruct((group, row_dev, width), jnp.bfloat16),
            ),
            in_specs=[any_space] * 8,
            out_specs=(vmem,) * 4,
            scratch_shapes=[
                pltpu.VMEM((tokens, width), jnp.bfloat16),
                pltpu.VMEM((tokens, width), jnp.bfloat16),
                pltpu.VMEM((tokens, width), jnp.bfloat16),
                pltpu.VMEM((1, width), jnp.float32),
                pltpu.VMEM((rows, tokens), jnp.bfloat16),
                pltpu.VMEM((rows, tokens), jnp.bfloat16),
                pltpu.VMEM((3, row_dev, width), jnp.float32),
                pltpu.VMEM((4, tokens, LANES), jnp.float32),
                pltpu.VMEM((2, half, width), jnp.float32),
                pltpu.VMEM((2, half, width), jnp.float32),
                pltpu.VMEM((2, half, width), jnp.float32),
                pltpu.VMEM((2, chips, row_dev, width), jnp.bfloat16),
                pltpu.VMEM((chips, row_dev, width), jnp.bfloat16),
                dma((11,)),
                dma((3,)),
                dma,
                dma,
                dma((2, CHUNKS)),
                dma((2, CHUNKS)),
                dma((2, chips, CHUNKS)),
                dma((chips, CHUNKS)),
                dma((chips, CHUNKS)),
                dma((chips, CHUNKS)),
                dma((chips, CHUNKS)),
                dma((chips, CHUNKS)),
            ],
            compiler_params=pltpu.CompilerParams(
                collective_id=0, has_side_effects=True, vmem_limit_bytes=60 * 2**20
            ),
        )(
            ln_input[0],
            ln_grad[0],
            top_grad[0],
            ln_gain,
            hidden[0].T,
            master[0],
            moment[0],
            second[0],
        )
        masters, moments, seconds, gathered = outs
        weights = gathered.reshape(rows, width)
        return (masters[None], moments[None], seconds[None], weights[None])

    return jax.shard_map(
        step,
        mesh=mesh,
        in_specs=(
            P("section", "dp", None),
            P("section", "dp", None),
            P("section", "dp", None),
            P("section", None),
            P("section", "dp", None),
            P("section", "dp", None),
            P("section", "dp", None),
            P("section", "dp", None),
        ),
        out_specs=(
            P("section", "dp", None),
            P("section", "dp", None),
            P("section", "dp", None),
            P("section", None, None),
        ),
        check_vma=False,
    )
```

time: 169 us -> 54.4 us (0.32)
  the two profiles are of different devices: /device:TPU:0 before, /device:TPU:7 now
where the time goes in v1:
time: 54.4 us; the launch traced here: 54.2 us
  Pallas kernels  46 us (85%)
  local copies, waits for them, and re-layouts  7.58 us (14%)
  between operations  0.64 us (1%)
    pallas_call x1, Pallas kernels, step(): pl.pallas_call(functools.partial(kernel, sections, group), out_shape=(sta...  46 us
    unnamed x3, local copies, waits for them, and re-layouts  4.62 us
    another operation x1, local copies, waits for them, and re-layouts, step(): return (masters[None], moments[None], seconds[None], weights[None])  2.96 us

profile of v1, /device:TPU:7, one launch (start us, length us, event | category | flops | bytes accessed | tf_op | source)
XLA Modules:
  0.0 54.2 jit_solution(9003215105501579780)
XLA Ops:
  0.6 46.0 %shard_map.111 = (f32[2,12288]{1,0:T(2,128)}, f32[2,12288]{1,0:T(2,128)}, f32[2,12288]{1,0:T(2,128)}, bf16[16,2,12288]{2,1,0:T(2,128)(2,1)}) custom-call(bf16[128,12288]{1,0:T(8,128)(2,1)} %bitcast.12, bf16[128,12288]{1,0:T(8,128)(2,1)} %bitcast.13, bf16[128,12288]{1,0:T(8,128)(2,1)} %bitcast.14, f32[1,12288]{1,0:T(1,128)} %gain_hbm.1, ...), custom_call_target="tpu_custom_call" | custom-call | tf_op jit(solution)/shard_map/pallas_call | solution.py:434
  46.6 3.0 %broadcast_in_dim_reshape.3 = bf16[1,32,12288]{2,1,0:T(8,128)(2,1)} reshape(bf16[16,2,12288]{2,1,0:T(2,128)(2,1)} %get-tuple-element.11) | data formatting | bytes 1572864 | tf_op jit(solution)/shard_map/broadcast_in_dim;reshape | solution.py:486
  49.6 1.5 %copy.15 = f32[1,2,12288]{2,1,0:T(2,128)} copy(f32[1,2,12288]{2,1,0:T(2,128)} %bitcast.20) | data formatting | bytes 196608
  51.1 1.5 %copy.16 = f32[1,2,12288]{2,1,0:T(2,128)} copy(f32[1,2,12288]{2,1,0:T(2,128)} %bitcast.19) | data formatting | bytes 196608
  52.6 1.5 %copy.17 = f32[1,2,12288]{2,1,0:T(2,128)} copy(f32[1,2,12288]{2,1,0:T(2,128)} %bitcast.18) | data formatting | bytes 196608

commit v2 on v1

--- a/solution.py
+++ b/solution.py
@@ -27,6 +27,7 @@
 def kernel(
     sections,
     group,
+    inner,
     ln_input_hbm,
     ln_grad_hbm,
     top_grad_hbm,
@@ -147,20 +148,20 @@
         device_id_type=MESH,
     )
 
+    @pl.when(is_last)
+    def _():
+        hidden_load.start()
+
+    @pl.when(has_lower | is_last)
+    def _():
+        t_load.start()
+
     @pl.when(has_lower)
     def _():
         gain_load.start()
         for b in range(blocks):
             x_loads[b].start()
             g_loads[b].start()
-
-    @pl.when(has_lower | is_last)
-    def _():
-        t_load.start()
-
-    @pl.when(is_last)
-    def _():
-        hidden_load.start()
 
     for load in state_loads:
         load.start()
@@ -249,9 +250,20 @@
         for step in range(1 if path == 1 else 0, chips):
             share_copy(path, q, other_chip(step)).start()
 
-    @pl.when(has_lower)
-    def _():
-        gain_load.wait()
+    @pl.when(has_lower | is_last)
+    def _():
+        t_load.wait()
+
+    @pl.when(is_last)
+    def _():
+        hidden_load.wait()
+        lhs = arranged(hidden_ref)
+        for q in range(CHUNKS):
+            product(1, q, lhs, lambda cols: t_ref[:, cols])
+            if q:
+                reduce_send(1, q - 1)
+
+    def statistics_of(first_block, last_block):
         sub_rows = 16
         span = 1536
 
@@ -296,14 +308,23 @@
             return carry
 
         per_block = block_rows // sub_rows
-        for b in range(blocks):
+        for b in range(first_block, last_block):
             x_loads[b].wait()
             g_loads[b].wait()
             lax.fori_loop(b * per_block, (b + 1) * per_block, statistics, 0)
 
-    @pl.when(has_lower | is_last)
-    def _():
-        t_load.wait()
+    @pl.when(has_lower)
+    def _():
+        gain_load.wait()
+        statistics_of(0, 1)
+
+    @pl.when(is_last)
+    def _():
+        reduce_send(1, CHUNKS - 1)
+
+    @pl.when(has_lower)
+    def _():
+        statistics_of(1, blocks)
 
     @pl.when(has_lower)
     def _():
@@ -325,22 +346,12 @@
                 reduce_send(0, q - 1)
         reduce_send(0, CHUNKS - 1)
 
-    @pl.when(is_last)
-    def _():
-        hidden_load.wait()
-        lhs = arranged(hidden_ref)
-        for q in range(CHUNKS):
-            product(1, q, lhs, lambda cols: t_ref[:, cols])
-            if q:
-                reduce_send(1, q - 1)
-        reduce_send(1, CHUNKS - 1)
-
     def gather_copy(q, source, target):
         cols = pl.ds(q * cols_chunk, cols_chunk)
         return pltpu.make_async_remote_copy(
             src_ref=weights_ref.at[chip_dev(source), :, cols],
             dst_ref=weights_ref.at[chip_dev(source), :, cols],
-            send_sem=ag_send.at[target, q],
+            send_sem=ag_send.at[lax.div(source, inner), target, q],
             recv_sem=ag_recv.at[source, q],
             device_id=(sec, chip_dev(target)),
             device_id_type=MESH,
@@ -355,6 +366,16 @@
             recv_sem=fw_recv.at[source, q],
             device_id=(sec, partner),
             device_id_type=MESH,
+        )
+
+    outer = chips // inner
+    my_outer = lax.div(chip, inner)
+    my_inner = lax.rem(chip, inner)
+
+    def at_chip(outer_step, inner_step):
+        return (
+            lax.rem(my_outer + outer_step, outer) * inner
+            + lax.rem(my_inner + inner_step, inner)
         )
 
     for load in state_loads:
@@ -381,22 +402,34 @@
             return carry
 
         lax.fori_loop(0, cols_chunk // part, update, 0)
-        for step in range(1, chips):
-            gather_copy(q, chip, other_chip(step)).start()
+        for step in range(1, outer):
+            gather_copy(q, chip, at_chip(step, 0)).start()
+        for step in range(1, inner):
+            gather_copy(q, chip, at_chip(0, step)).start()
         forward_copy(q, chip).start()
 
     for q in range(CHUNKS):
-        for step in range(1, chips):
-            source = other_chip(step)
+        for outer_step in range(1, outer):
+            source = at_chip(outer_step, 0)
             gather_copy(q, source, chip).wait_recv()
+            for step in range(1, inner):
+                gather_copy(q, source, at_chip(0, step)).start()
             forward_copy(q, source).start()
-
     for q in range(CHUNKS):
-        for step in range(chips):
-            source = other_chip(step)
-            forward_copy(q, source).wait()
-            if step:
-                gather_copy(q, chip, source).wait_send()
+        for outer_step in range(outer):
+            for step in range(1, inner):
+                source = at_chip(outer_step, step)
+                gather_copy(q, source, chip).wait_recv()
+                forward_copy(q, source).start()
+
+    for q in range(CHUNKS):
+        for outer_step in range(outer):
+            for step in range(inner):
+                forward_copy(q, at_chip(outer_step, step)).wait()
+            for step in range(1, inner):
+                gather_copy(q, at_chip(outer_step, 0), at_chip(0, step)).wait_send()
+            if outer_step:
+                gather_copy(q, chip, at_chip(outer_step, 0)).wait_send()
 
     def finish(path):
         for q in range(CHUNKS):
@@ -417,10 +450,22 @@
         hidden_copy.wait_send()
 
 
+def write_out(master, moment, second, gathered, new_master, new_moment, new_second, weights):
+    new_master[...] = master[...]
+    new_moment[...] = moment[...]
+    new_second[...] = second[...]
+    group, row_dev, _ = gathered.shape
+    for owner in range(group):
+        weights[owner * row_dev : (owner + 1) * row_dev] = gathered[owner]
+
+
 def solution(mesh):
     sections = mesh.shape["section"]
     group = mesh.shape["dp"]
     chips = group // CORES
+    inner = 1
+    while inner * inner * 4 <= chips and chips % (inner * 2) == 0:
+        inner *= 2
 
     def step(ln_input, ln_grad, top_grad, ln_gain, hidden, master, moment, second):
         tokens, width = ln_input.shape[1:]
@@ -432,7 +477,7 @@
         state = jax.ShapeDtypeStruct((row_dev, width), jnp.float32)
         dma = pltpu.SemaphoreType.DMA
         outs = pl.pallas_call(
-            functools.partial(kernel, sections, group),
+            functools.partial(kernel, sections, group, inner),
             out_shape=(
                 state,
                 state,
@@ -463,7 +508,7 @@
                 dma((2, CHUNKS)),
                 dma((2, chips, CHUNKS)),
                 dma((chips, CHUNKS)),
-                dma((chips, CHUNKS)),
+                dma((chips // inner, chips, CHUNKS)),
                 dma((chips, CHUNKS)),
                 dma((chips, CHUNKS)),
                 dma((chips, CHUNKS)),
@@ -481,8 +526,15 @@
             moment[0],
             second[0],
         )
-        masters, moments, seconds, gathered = outs
-        weights = gathered.reshape(rows, width)
+        slab = width // 4
+        strip = pl.BlockSpec((row_dev, slab), lambda i: (0, i))
+        masters, moments, seconds, weights = pl.pallas_call(
+            write_out,
+            grid=(width // slab,),
+            out_shape=(state, state, state, jax.ShapeDtypeStruct((rows, width), jnp.bfloat16)),
+            in_specs=[strip] * 3 + [pl.BlockSpec((group, row_dev, slab), lambda i: (0, 0, i))],
+            out_specs=(strip,) * 3 + (pl.BlockSpec((rows, slab), lambda i: (0, i)),),
+        )(*outs)
         return (masters[None], moments[None], seconds[None], weights[None])
 
     return jax.shard_map(

time: 54.4 us -> 51.7 us (0.950)
  the two profiles are of different devices: /device:TPU:7 before, /device:TPU:0 now
where the time goes in v2:
time: 51.7 us; the launch traced here: 51.5 us
  Pallas kernels  50.8 us (98%)
  between operations  0.64 us (1%)
    pallas_call x1, Pallas kernels, step(): pl.pallas_call(functools.partial(kernel, sections, group, inner), out_sha...  47.3 us
    pallas_call x1, Pallas kernels, step(): pl.pallas_call(write_out, grid=(width // slab,), out_shape=(state, state,...  3.58 us

profile of v2, /device:TPU:0, one launch (start us, length us, event | category | flops | bytes accessed | tf_op | source)
XLA Modules:
  0.0 51.5 jit_solution(8649474567509259168)
XLA Ops:
  0.6 47.3 %shard_map.111 = (f32[2,12288]{1,0:T(2,128)}, f32[2,12288]{1,0:T(2,128)}, f32[2,12288]{1,0:T(2,128)}, bf16[16,2,12288]{2,1,0:T(2,128)(2,1)}) custom-call(bf16[128,12288]{1,0:T(8,128)(2,1)} %bitcast.13, bf16[128,12288]{1,0:T(8,128)(2,1)} %bitcast.14, bf16[128,12288]{1,0:T(8,128)(2,1)} %bitcast.15, f32[1,12288]{1,0:T(1,128)} %gain_hbm.1, ...), custom_call_target="tpu_custom_call" | custom-call | tf_op jit(solution)/shard_map/pallas_call | solution.py:479
  47.9 3.6 %shard_map.112 = (f32[2,12288]{1,0:T(2,128)}, f32[2,12288]{1,0:T(2,128)}, f32[2,12288]{1,0:T(2,128)}, bf16[32,12288]{1,0:T(8,128)(2,1)}) custom-call(f32[2,12288]{1,0:T(2,128)} %get-tuple-element.12.master, f32[2,12288]{1,0:T(2,128)} %get-tuple-element.13.moment, f32[2,12288]{1,0:T(2,128)} %get-tuple-element.14.second, ...), custom_call_target="tpu_custom_call" | custom-call | tf_op jit(solution)/shard_map/pallas_call | solution.py:531

commit v3 on v2

--- a/solution.py
+++ b/solution.py
@@ -43,6 +43,7 @@
     x_ref,
     g_ref,
     t_ref,
+    passed_ref,
     gain_ref,
     hidden_ref,
     lower_ref,
@@ -52,6 +53,9 @@
     theirs_ref,
     partner_ref,
     stage_ref,
+    base_ref,
+    side_ref,
+    part_ref,
     recv_ref,
     load_sem,
     state_sem,
@@ -59,8 +63,12 @@
     hid_recv,
     pair_send,
     pair_recv,
-    rs_send,
-    rs_recv,
+    down_send,
+    down_recv,
+    inner_send,
+    inner_recv,
+    outer_send,
+    outer_recv,
     ag_send,
     ag_recv,
     fw_send,
@@ -87,35 +95,34 @@
     def chip_dev(index):
         return index * CORES + core
 
-    def other_chip(step):
-        return lax.rem(chip + step, chips)
+    outer = chips // inner
+    my_outer = lax.div(chip, inner)
+    my_inner = lax.rem(chip, inner)
+
+    def at_chip(outer_step, inner_step):
+        return (
+            lax.rem(my_outer + outer_step, outer) * inner
+            + lax.rem(my_inner + inner_step, inner)
+        )
 
     barrier = pltpu.get_barrier_semaphore()
     pl.semaphore_signal(barrier, inc=1, device_id=(sec, partner), device_id_type=MESH)
-    for step in range(1, chips):
+    for step in range(1, outer):
         pl.semaphore_signal(
-            barrier, inc=1, device_id=(sec, chip_dev(other_chip(step))), device_id_type=MESH
+            barrier, inc=1, device_id=(sec, chip_dev(at_chip(step, 0))), device_id_type=MESH
+        )
+    for step in range(1, inner):
+        pl.semaphore_signal(
+            barrier, inc=1, device_id=(sec, chip_dev(at_chip(0, step))), device_id_type=MESH
         )
 
     @pl.when(has_lower)
     def _():
-        for step in range(chips):
-            pl.semaphore_signal(
-                barrier,
-                inc=1,
-                device_id=(sec - 1, chip_dev(other_chip(step))),
-                device_id_type=MESH,
-            )
+        pl.semaphore_signal(barrier, inc=1, device_id=(sec - 1, me), device_id_type=MESH)
 
     @pl.when(has_upper)
     def _():
-        for step in range(chips):
-            pl.semaphore_signal(
-                barrier,
-                inc=1,
-                device_id=(sec + 1, chip_dev(other_chip(step))),
-                device_id_type=MESH,
-            )
+        pl.semaphore_signal(barrier, inc=1, device_id=(sec + 1, me), device_id_type=MESH)
 
     def row_block(b):
         return pl.ds(b * block_rows, block_rows)
@@ -152,10 +159,6 @@
     def _():
         hidden_load.start()
 
-    @pl.when(has_lower | is_last)
-    def _():
-        t_load.start()
-
     @pl.when(has_lower)
     def _():
         gain_load.start()
@@ -163,13 +166,19 @@
             x_loads[b].start()
             g_loads[b].start()
 
+    @pl.when(has_lower | is_last)
+    def _():
+        t_load.start()
+
     for load in state_loads:
         load.start()
 
     peers = (
-        chips
-        + jnp.where(has_lower, chips, 0)
-        + jnp.where(has_upper, chips, 0)
+        outer
+        + inner
+        - 1
+        + jnp.where(has_lower, 1, 0)
+        + jnp.where(has_upper, 1, 0)
     )
     pl.semaphore_wait(barrier, peers)
 
@@ -185,7 +194,9 @@
         at = lax.broadcasted_iota(jnp.int32, (rows, rows), 1)
         within = lax.rem(to, half)
         which = jnp.where(to < half, core, 1 - core)
-        wanted = (lax.div(within, row_dev) * CORES + which) * row_dev + lax.rem(within, row_dev)
+        place = lax.div(within, row_dev)
+        owner = lax.rem(place, outer) * inner + lax.div(place, outer)
+        wanted = (owner * CORES + which) * row_dev + lax.rem(within, row_dev)
         select = jnp.where(at == wanted, 1.0, 0.0).astype(jnp.bfloat16)
         return lax.dot_general(
             select, source[...], (((1,), (0,)), ((), ())), preferred_element_type=jnp.float32
@@ -202,70 +213,100 @@
             device_id_type=MESH,
         )
 
-    def share_copy(path, q, target):
-        cols = pl.ds(q * cols_chunk, cols_chunk)
-        to_sec = lax.rem(sec + sections - 1, sections) if path == 0 else sec
+    def down_copy(q):
+        cols = pl.ds(q * cols_chunk, cols_chunk)
         return pltpu.make_async_remote_copy(
-            src_ref=stage_ref.at[path, target, :, cols],
-            dst_ref=recv_ref.at[chip, :, cols],
-            send_sem=rs_send.at[path, target, q],
-            recv_sem=rs_recv.at[chip, q],
-            device_id=(to_sec, chip_dev(target)),
+            src_ref=stage_ref.at[:, :, cols],
+            dst_ref=base_ref.at[:, :, cols],
+            send_sem=down_send.at[q],
+            recv_sem=down_recv.at[q],
+            device_id=(lax.rem(sec + sections - 1, sections), me),
             device_id_type=MESH,
         )
 
+    def inner_copy(q, source, step):
+        cols = pl.ds(q * cols_chunk, cols_chunk)
+        target = lax.rem(my_inner + step, inner)
+        return pltpu.make_async_remote_copy(
+            src_ref=base_ref.at[pl.ds(target * outer, outer), :, cols],
+            dst_ref=side_ref.at[source, :, :, cols],
+            send_sem=inner_send.at[target, q],
+            recv_sem=inner_recv.at[source, q],
+            device_id=(sec, chip_dev(at_chip(0, step))),
+            device_id_type=MESH,
+        )
+
+    def outer_copy(q, source, step):
+        cols = pl.ds(q * cols_chunk, cols_chunk)
+        target = lax.rem(my_outer + step, outer)
+        return pltpu.make_async_remote_copy(
+            src_ref=part_ref.at[target, :, cols],
+            dst_ref=recv_ref.at[source, :, cols],
+            send_sem=outer_send.at[target, q],
+            recv_sem=outer_recv.at[source, q],
+            device_id=(sec, chip_dev(at_chip(step, 0))),
+            device_id_type=MESH,
+        )
+
     def own_copy(q):
         cols = pl.ds(q * cols_chunk, cols_chunk)
         return pltpu.make_async_copy(
-            stage_ref.at[1, chip, :, cols], recv_ref.at[chip, :, cols], rs_recv.at[chip, q]
-        )
-
-    sub = 256
-
-    def product(path, q, lhs, make):
+            part_ref.at[my_outer, :, cols],
+            recv_ref.at[my_outer, :, cols],
+            outer_recv.at[my_outer, q],
+        )
+
+    def send_inner(q):
+        for step in range(1, inner):
+            inner_copy(q, my_inner, step).start()
+
+    def add_inner(q):
+        for step in range(1, inner):
+            inner_copy(q, lax.rem(my_inner + step, inner), step).wait_recv()
+        part = cols_chunk // 2
+
         def body(i, carry):
-            cols = columns(q * cols_chunk + i * sub, sub)
-            term = jnp.dot(lhs, make(cols), preferred_element_type=jnp.float32)
-            mine_ref[path, :, cols] = term[:half]
-            theirs_ref[path, :, cols] = term[half:]
+            cols = columns(q * cols_chunk + i * part, part)
+            total = base_ref[pl.ds(my_inner * outer, outer), :, cols].astype(jnp.float32)
+            for step in range(1, inner):
+                total += side_ref[lax.rem(my_inner + step, inner), :, :, cols].astype(jnp.float32)
+            part_ref[:, :, cols] = total.astype(jnp.bfloat16)
             return carry
 
-        lax.fori_loop(0, cols_chunk // sub, body, 0)
+        lax.fori_loop(0, cols_chunk // part, body, 0)
+        own_copy(q).start()
+        for step in range(1, outer):
+            outer_copy(q, my_outer, step).start()
+
+    def product(path, q, lhs):
+        cols = pl.ds(q * cols_chunk, cols_chunk)
+        rhs = t_ref[:, cols] if path else passed_ref[...]
+        term = jnp.dot(lhs, rhs, preferred_element_type=jnp.float32)
+        mine_ref[path, :, cols] = term[:half]
+        theirs_ref[path, :, cols] = term[half:]
         pair_copy(path, q).start()
 
     def reduce_send(path, q):
         pair_copy(path, q).wait_recv()
-        part = 512
+        to_ref = base_ref if path else stage_ref
+        part = cols_chunk // 2
 
         def body(i, carry):
             cols = columns(q * cols_chunk + i * part, part)
             total = (mine_ref[path, :, cols] + partner_ref[path, :, cols]).astype(jnp.bfloat16)
             for k in range(chips):
-                stage_ref[path, k, :, cols] = total[k * row_dev : (k + 1) * row_dev]
+                to_ref[k, :, cols] = total[k * row_dev : (k + 1) * row_dev]
             return carry
 
         lax.fori_loop(0, cols_chunk // part, body, 0)
-        if path == 1:
-            own_copy(q).start()
-        for step in range(1 if path == 1 else 0, chips):
-            share_copy(path, q, other_chip(step)).start()
-
-    @pl.when(has_lower | is_last)
-    def _():
-        t_load.wait()
-
-    @pl.when(is_last)
-    def _():
-        hidden_load.wait()
-        lhs = arranged(hidden_ref)
-        for q in range(CHUNKS):
-            product(1, q, lhs, lambda cols: t_ref[:, cols])
-            if q:
-                reduce_send(1, q - 1)
+        if path == 0:
+            down_copy(q).start()
+        else:
+            send_inner(q)
 
     def statistics_of(first_block, last_block):
-        sub_rows = 16
-        span = 1536
+        sub_rows = 32
+        span = cols_chunk // 2
 
         def fold(value):
             parts = [value[:, i * LANES : (i + 1) * LANES] for i in range(span // LANES)]
@@ -316,35 +357,54 @@
     @pl.when(has_lower)
     def _():
         gain_load.wait()
-        statistics_of(0, 1)
-
-    @pl.when(is_last)
-    def _():
-        reduce_send(1, CHUNKS - 1)
-
-    @pl.when(has_lower)
-    def _():
-        statistics_of(1, blocks)
+        statistics_of(0, blocks)
+
+    @pl.when(has_lower | is_last)
+    def _():
+        t_load.wait()
 
     @pl.when(has_lower)
     def _():
         hidden_copy.wait_recv()
         lhs = arranged(lower_ref)
 
-        def passed(cols):
-            def wide(i):
-                return jnp.concatenate([stats_ref[i]] * (sub // LANES), axis=1)
-
-            centred = x_ref[:, cols].astype(jnp.float32) - wide(0)
-            scaled = g_ref[:, cols].astype(jnp.float32) * gain_ref[:, cols]
-            inner = (scaled - wide(1)) - centred * wide(2)
-            return (t_ref[:, cols].astype(jnp.float32) + inner * wide(3)).astype(jnp.bfloat16)
+        span = cols_chunk // 2
+        pass_rows = 32
+
+        def passed(q):
+            def body(i, carry):
+                at = pl.ds(pl.multiple_of(lax.rem(i, tokens // pass_rows) * pass_rows, pass_rows), pass_rows)
+                cols = columns(q * cols_chunk + lax.div(i, tokens // pass_rows) * span, span)
+
+                def wide(which):
+                    return jnp.concatenate([stats_ref[which, at]] * (span // LANES), axis=1)
+
+                centred = x_ref[at, cols].astype(jnp.float32) - wide(0)
+                scaled = g_ref[at, cols].astype(jnp.float32) * gain_ref[:, cols]
+                inner_term = (scaled - wide(1)) - centred * wide(2)
+                passed_ref[at, pl.ds(pl.multiple_of(lax.div(i, tokens // pass_rows) * span, LANES), span)] = (
+                    t_ref[at, cols].astype(jnp.float32) + inner_term * wide(3)
+                ).astype(jnp.bfloat16)
+                return carry
+
+            lax.fori_loop(0, tokens // pass_rows * (cols_chunk // span), body, 0)
 
         for q in range(CHUNKS):
-            product(0, q, lhs, passed)
+            passed(q)
+            product(0, q, lhs)
             if q:
                 reduce_send(0, q - 1)
         reduce_send(0, CHUNKS - 1)
+
+    @pl.when(is_last)
+    def _():
+        hidden_load.wait()
+        lhs = arranged(hidden_ref)
+        for q in range(CHUNKS):
+            product(1, q, lhs)
+            if q:
+                reduce_send(1, q - 1)
+        reduce_send(1, CHUNKS - 1)
 
     def gather_copy(q, source, target):
         cols = pl.ds(q * cols_chunk, cols_chunk)
@@ -368,26 +428,16 @@
             device_id_type=MESH,
         )
 
-    outer = chips // inner
-    my_outer = lax.div(chip, inner)
-    my_inner = lax.rem(chip, inner)
-
-    def at_chip(outer_step, inner_step):
-        return (
-            lax.rem(my_outer + outer_step, outer) * inner
-            + lax.rem(my_inner + inner_step, inner)
-        )
-
     for load in state_loads:
         load.wait()
 
-    for q in range(CHUNKS):
-        cols = pl.ds(q * cols_chunk, cols_chunk)
-        for k in range(chips):
+    def finish_chunk(q):
+        cols = pl.ds(q * cols_chunk, cols_chunk)
+        for k in range(outer):
             pltpu.make_async_copy(
-                recv_ref.at[k, :, cols], recv_ref.at[k, :, cols], rs_recv.at[k, q]
+                recv_ref.at[k, :, cols], recv_ref.at[k, :, cols], outer_recv.at[k, q]
             ).wait()
-        part = 512
+        part = cols_chunk // 2
 
         def update(i, carry):
             at = columns(q * cols_chunk + i * part, part)
@@ -407,6 +457,20 @@
         for step in range(1, inner):
             gather_copy(q, chip, at_chip(0, step)).start()
         forward_copy(q, chip).start()
+
+    for turn in range(CHUNKS + 2):
+
+        if turn < CHUNKS:
+
+            @pl.when(has_upper)
+            def _():
+                down_copy(turn).wait_recv()
+                send_inner(turn)
+
+        if 0 < turn <= CHUNKS:
+            add_inner(turn - 1)
+        if turn >= 2:
+            finish_chunk(turn - 2)
 
     for q in range(CHUNKS):
         for outer_step in range(1, outer):
@@ -434,8 +498,14 @@
     def finish(path):
         for q in range(CHUNKS):
             pair_copy(path, q).wait_send()
-            for step in range(1 if path == 1 else 0, chips):
-                share_copy(path, q, other_chip(step)).wait_send()
+            if path == 0:
+                down_copy(q).wait_send()
+
+    for q in range(CHUNKS):
+        for step in range(1, inner):
+            inner_copy(q, my_inner, step).wait_send()
+        for step in range(1, outer):
+            outer_copy(q, my_outer, step).wait_send()
 
     @pl.when(has_lower)
     def _():
@@ -490,6 +560,7 @@
                 pltpu.VMEM((tokens, width), jnp.bfloat16),
                 pltpu.VMEM((tokens, width), jnp.bfloat16),
                 pltpu.VMEM((tokens, width), jnp.bfloat16),
+                pltpu.VMEM((tokens, width // CHUNKS), jnp.bfloat16),
                 pltpu.VMEM((1, width), jnp.float32),
                 pltpu.VMEM((rows, tokens), jnp.bfloat16),
                 pltpu.VMEM((rows, tokens), jnp.bfloat16),
@@ -498,16 +569,23 @@
                 pltpu.VMEM((2, half, width), jnp.float32),
                 pltpu.VMEM((2, half, width), jnp.float32),
                 pltpu.VMEM((2, half, width), jnp.float32),
-                pltpu.VMEM((2, chips, row_dev, width), jnp.bfloat16),
                 pltpu.VMEM((chips, row_dev, width), jnp.bfloat16),
+                pltpu.VMEM((chips, row_dev, width), jnp.bfloat16),
+                pltpu.VMEM((inner, chips // inner, row_dev, width), jnp.bfloat16),
+                pltpu.VMEM((chips // inner, row_dev, width), jnp.bfloat16),
+                pltpu.VMEM((chips // inner, row_dev, width), jnp.bfloat16),
                 dma((11,)),
                 dma((3,)),
                 dma,
                 dma,
                 dma((2, CHUNKS)),
                 dma((2, CHUNKS)),
-                dma((2, chips, CHUNKS)),
-                dma((chips, CHUNKS)),
+                dma((CHUNKS,)),
+                dma((CHUNKS,)),
+                dma((inner, CHUNKS)),
+                dma((inner, CHUNKS)),
+                dma((chips // inner, CHUNKS)),
+                dma((chips // inner, CHUNKS)),
                 dma((chips // inner, chips, CHUNKS)),
                 dma((chips, CHUNKS)),
                 dma((chips, CHUNKS)),
@@ -526,7 +604,7 @@
             moment[0],
             second[0],
         )
-        slab = width // 4
+        slab = width // 2
         strip = pl.BlockSpec((row_dev, slab), lambda i: (0, i))
         masters, moments, seconds, weights = pl.pallas_call(
             write_out,

time: 51.7 us -> 45.1 us (0.87)
  Pallas kernels: 50.8 us -> 44.3 us
    pallas_call x1, Pallas kernels: 47.3 us -> 42 us  [step(): pl.pallas_call(functools.partial(kernel, sections, group, inner), out_sha...]
    pallas_call x1, Pallas kernels: 3.58 us -> 2.32 us  [step(): pl.pallas_call(write_out, grid=(width // slab,), out_shape=(state, state,...]
where the time goes in v3:
time: 45.1 us; the launch traced here: 44.9 us
  Pallas kernels  44.3 us (98%)
  between operations  0.64 us (1%)
    pallas_call x1, Pallas kernels, step(): pl.pallas_call(functools.partial(kernel, sections, group, inner), out_sha...  42 us
    pallas_call x1, Pallas kernels, step(): pl.pallas_call(write_out, grid=(width // slab,), out_shape=(state, state,...  2.32 us

profile of v3, /device:TPU:0, one launch (start us, length us, event | category | flops | bytes accessed | tf_op | source)
XLA Modules:
  0.0 44.9 jit_solution(5197778454789284417)
XLA Ops:
  0.6 42.0 %shard_map.111 = (f32[2,12288]{1,0:T(2,128)}, f32[2,12288]{1,0:T(2,128)}, f32[2,12288]{1,0:T(2,128)}, bf16[16,2,12288]{2,1,0:T(2,128)(2,1)}) custom-call(bf16[128,12288]{1,0:T(8,128)(2,1)} %bitcast.13, bf16[128,12288]{1,0:T(8,128)(2,1)} %bitcast.14, bf16[128,12288]{1,0:T(8,128)(2,1)} %bitcast.15, f32[1,12288]{1,0:T(1,128)} %gain_hbm.1, ...), custom_call_target="tpu_custom_call" | custom-call | tf_op jit(solution)/shard_map/pallas_call | solution.py:549
  42.6 2.3 %shard_map.112 = (f32[2,12288]{1,0:T(2,128)}, f32[2,12288]{1,0:T(2,128)}, f32[2,12288]{1,0:T(2,128)}, bf16[32,12288]{1,0:T(8,128)(2,1)}) custom-call(f32[2,12288]{1,0:T(2,128)} %get-tuple-element.12.master, f32[2,12288]{1,0:T(2,128)} %get-tuple-element.13.moment, f32[2,12288]{1,0:T(2,128)} %get-tuple-element.14.second, ...), custom_call_target="tpu_custom_call" | custom-call | tf_op jit(solution)/shard_map/pallas_call | solution.py:609
